TPU v7x, 32 devices: a whole 2x2x4 slice. The times are simulated.
32 devices in a mesh: pairs: 8 (over z, y), cols: 4 (over x, core).
Axes of the slice: x: 2, y: 2, z: 4, core: 2. Of those that a mesh axis runs over, the one named last changes fastest.
Arguments:
- amplitudes: bfloat16 [64, 256, 256], P('pairs', 'cols'), may hold values from -6 to 6
- pno_counts: int32 [64], P('pairs'), may hold values from 96 to 256
- fock_blocks: bfloat16 [64, 256, 256], P('pairs'), may hold values from -1 to 5, as said below
- exchange_blocks: bfloat16 [64, 256, 256], P('pairs', 'cols'), may hold values from -6 to 6
- intersections: bfloat16 [64, 32, 256, 256], P('pairs', None, 'cols'), may hold values from -0.375 to 0.375
- partners: int32 [64, 32], P('pairs'), may hold values from 0 to 63, as said below
- couplings: float32 [64, 32], P('pairs'), may hold values from -3 to 3
Outputs:
- residual_blocks: bfloat16 [64, 256, 256], P('pairs', 'cols')
Inputs may be any that keep to these rules, and one draw needn't show every extreme that they name: `partners`: within the coupling lists of one aligned block of 8 pairs, at most 64 entries name pairs of any one aligned block of 8 pairs, and exactly 64 do for some block. `fock_blocks`: each block is symmetric.
All inputs are finite; a program needn't handle non-finite values.
Results may differ from a plain program's by a relative error of at most 0.0022.
Values may be sent and summed in bfloat16 or wider, within the bound.
No kernel may reach another device: no remote copies, remote signals or barrier semaphores. Data moves between devices by JAX's collectives and lax.ppermute only.
A program may use at most 128 MiB of HBM per device.

v0:
```python
import jax
import jax.numpy as jnp
from jax import lax
from jax.sharding import PartitionSpec as P

CPL = 32


def shards(
    amplitudes, pno_counts, fock_blocks, exchange_blocks, intersections, partners, couplings
):
    local_pairs, share, width = amplitudes.shape
    column = lax.axis_index("cols")
    row_keep = column * share + jnp.arange(share, dtype=jnp.int32)[None, :] < pno_counts[:, None]
    col_keep = jnp.arange(width, dtype=jnp.int32)[None, :] < pno_counts[:, None]
    keep = row_keep[:, :, None] & col_keep[:, None, :]
    masked = jnp.where(keep, amplitudes, jnp.zeros_like(amplitudes))
    linear = partners.reshape(-1)
    empty = jnp.zeros((local_pairs * CPL, share, width), jnp.bfloat16)
    piece = lax.all_gather(masked, "pairs", axis=0, tiled=True)
    present = (linear >= 0) & (linear < piece.shape[0])
    picked = piece[jnp.clip(linear, 0, piece.shape[0] - 1)]
    partner_flat = jnp.where(present[:, None, None], picked, empty)
    partner_blocks = partner_flat.reshape(local_pairs, CPL, share, width)
    fock_cols = lax.dynamic_slice_in_dim(fock_blocks, column * share, share, 2)
    partial_value = jnp.einsum(
        "pab,pbc->pac", fock_cols, masked, preferred_element_type=jnp.float32
    )
    whole_intersections = lax.all_gather(intersections, "cols", axis=2, tiled=True)
    projected = jnp.einsum(
        "pqab,pqbc->pqac", partner_blocks, whole_intersections, preferred_element_type=jnp.float32
    ).astype(jnp.bfloat16)
    for slot_index in range(CPL):
        term = jnp.einsum(
            "pcd,pca->pda",
            intersections[:, slot_index],
            projected[:, slot_index],
            preferred_element_type=jnp.float32,
        )
        partial_value = partial_value + couplings[:, slot_index, None, None] * term
    summed = lax.psum_scatter(partial_value, "cols", scatter_dimension=1, tiled=True)
    fock_term = jnp.einsum("pab,pbc->pac", masked, fock_blocks, preferred_element_type=jnp.float32)
    total = exchange_blocks.astype(jnp.float32) + fock_term + summed
    return jnp.where(keep, total, jnp.zeros_like(total)).astype(jnp.bfloat16)


def solution(mesh):
    in_specs = (
        P("pairs", "cols", None),
        P("pairs"),
        P("pairs", None, None),
        P("pairs", "cols", None),
        P("pairs", None, "cols", None),
        P("pairs", None),
        P("pairs", None),
    )
    out_specs = P("pairs", "cols", None)
    return jax.shard_map(shards, mesh=mesh, in_specs=in_specs, out_specs=out_specs, check_vma=False)
```

profile of v0, /device:TPU:0, one launch (start us, length us, event | category | flops | bytes accessed | tf_op | source)
XLA Modules:
  0.0 406.6 jit_solution(1802354815083428256)
XLA Ops:
  6.5 0.0 copy-start
  6.5 0.0 all-gather.3.cloned.1.call-start
  6.5 0.8 iota_compare_fusion
  7.4 0.7 broadcast_compare_fusion
  8.1 1.8 and_select_fusion
  9.9 0.0 all-gather.3.cloned.1.call-update
  9.9 0.0 copy-start.4
  9.9 0.0 copy-start.2
  9.9 0.0 all-gather.5.cloned.1.call-start
  10.0 0.7 all-gather.5.cloned.1.call-update
  10.7 0.0 reduce-scatter.2.cloned.1.call-start
  10.7 0.0 copy-done.4
  10.8 0.1 min.12
  10.8 0.0 copy-done.2
  10.9 0.4 slice_reduce_fusion.30
  11.3 0.5 slice_reduce_fusion.31
  11.7 50.1 %all-gather.3.cloned.1.call-done = bf16[64,64,256]{2,1,0:T(8,128)(2,1)} async-done(((bf16[8,64,256]{2,1,0:T(8,128)(2,1)}), bf16[64,64,256]{2,1,0:T(8,128)(2,1)}) %all-gather.3.cloned.1.call-update) | async-done | bytes 2097168 | tf_op jit(solution)/shard_map/all_gather | solution.py:20
  61.9 12.4 %gather_fusion = bf16[256,64,256]{2,1,0:T(8,128)(2,1)} fusion(bf16[64,64,256]{2,1,0:T(8,128)(2,1)} %all-gather.3.cloned.1.call-done, s32[1024]{0:T(1024)S(1)} %pad_clamp_fusion), kind=kCustom, calls=%fused_computation | custom fusion | bytes 16778240 | tf_op jit(solution)/shard_map/gather | solution.py:22
  74.2 189.3 %all-gather.5.cloned.1.call-done = bf16[8,32,256,256]{3,2,1,0:T(8,128)(2,1)} async-done(((bf16[8,32,64,256]{3,2,1,0:T(8,128)(2,1)}), bf16[8,32,256,256]{3,2,1,0:T(8,128)(2,1)}) %all-gather.5.cloned.1.call-update) | async-done | bytes 33554448 | tf_op jit(solution)/shard_map/all_gather | solution.py:29
  263.5 15.6 %fusion.3 = bf16[8,32,64,256]{3,2,1,0:T(8,128)(2,1)S(1)} fusion(bf16[8,32,256,256]{3,2,1,0:T(8,128)(2,1)} %all-gather.5.cloned.1.call-done, bf16[8,32,64,256]{3,2,1,0:T(8,128)(2,1)} %bitcast.390, pred[8,32]{1,0:T(8,128)(4,1)S(1)} %compare_and_fusion), kind=kOutput, calls=%fused_computation.4 | convolution fusion | flops 2155872256 | bytes 50331904 | tf_op jit(solution)/shard_map/pqab,pqbc->pqac/dot_general | solution.py:30
  279.1 0.0 slice-start
  279.1 2.9 fusion.11
  282.0 2.8 fusion.12
  284.8 2.7 fusion.13
  287.6 0.0 slice-start.1
  287.6 2.9 fusion.14
  290.5 2.8 fusion.15
  293.3 2.8 fusion.16
  296.1 0.0 slice-done
  296.1 0.0 slice-done.1
  296.1 1.8 fusion.17
  297.9 1.9 fusion.18
  299.7 1.8 fusion.19
  301.6 1.8 fusion.20
  303.4 1.8 fusion.21
  305.2 1.8 fusion.22
  307.0 1.8 fusion.23
  308.8 1.9 fusion.24
  310.7 1.8 fusion.25
  312.5 1.8 fusion.26
  314.3 1.8 fusion.27
  316.1 1.8 fusion.28
  317.9 1.9 fusion.29
  319.8 1.8 fusion.30
  321.6 1.8 fusion.31
  323.4 1.8 fusion.32
  325.2 1.8 fusion.33
  327.0 1.8 fusion.34
  328.8 1.8 fusion.35
  330.6 1.8 fusion.36
  332.4 1.9 fusion.37
  334.3 1.8 fusion.38
  336.1 1.8 fusion.39
  337.9 1.8 fusion.40
  339.7 1.8 fusion.41
  341.5 1.8 fusion.42
  343.3 0.0 copy-done
  343.3 0.0 copy-done.1
  343.3 23.3 %bitcast_add_fusion = f32[8,256,256]{2,1,0:T(8,128)} fusion(f32[8,256,256]{1,2,0:T(8,128)} %fusion.11, f32[8,256,256]{1,2,0:T(8,128)} %fusion.12, f32[8,256,256]{1,2,0:T(8,128)} %fusion.13, f32[8,256,256]{1,2,0:T(8,128)} %fusion.14, f32[8,256,256]{1,2,0:T(8,128)} %fusion.15, f32[8,256,256]{1,2,0:T(8,128)} %fusion.16, f32[8,256,256]{1,2,0:T(8,128)} %fusion.17, ...), kind=kOutput, calls=%fused_computation.6 | convolution fusion | flops 100663296 | bytes 70008832 | tf_op jit(solution)/shard_map/pab,pbc->pac/dot_general | solution.py:26
  366.6 0.0 copy-start.3
  366.6 0.0 reduce-scatter.2.cloned.1.call-update
  366.7 31.3 %reduce-scatter.2.cloned.1.call-done = f32[8,64,256]{2,1,0:T(8,128)} async-done(((f32[8,256,256]{2,1,0:T(8,128)}), f32[8,64,256]{2,1,0:T(8,128)}) %reduce-scatter.2.cloned.1.call-update) | async-done | bytes 524304 | tf_op jit(solution)/shard_map/reduce_scatter | solution.py:41
  398.0 0.0 copy-done.3
  398.0 2.1 fusion.9
  (7 shorter events, 0.0 us)
Async XLA Ops:
  6.5 336.8 %copy-start = (bf16[8,256,256]{2,1,0:T(8,128)(2,1)S(1)}, bf16[8,256,256]{2,1,0:T(8,128)(2,1)}, u32[]{:S(2)}) copy-start(bf16[8,256,256]{2,1,0:T(8,128)(2,1)} %param.9) | copy-start | bytes 3145732
  6.5 55.3 %all-gather.3.cloned.1.call-start = ((), (), s32[]{:S(2)}) async-start(), calls=%async_computation.1 | async-start | bytes 2359296 | tf_op jit(solution)/shard_map/all_gather | solution.py:20
  9.9 0.8 copy-start.4
  9.9 0.9 copy-start.2
  9.9 253.6 %all-gather.5.cloned.1.call-start = ((), (), s32[]{:S(2)}) async-start(), calls=%async_computation.2 | async-start | bytes 41943040 | tf_op jit(solution)/shard_map/all_gather | solution.py:29
  10.7 387.3 %reduce-scatter.2.cloned.1.call-start = ((), (), s32[]{:S(2)}) async-start(), calls=%async_computation.3 | async-start | bytes 2621440 | tf_op jit(solution)/shard_map/reduce_scatter | solution.py:41
  279.1 17.0 %slice-start = ((s8[8388608]{0:T(1024)(128)(4,1)}), s8[4194304]{0:T(1024)(128)(4,1)S(1)}, s32[]{:S(2)}) async-start(s8[8388608]{0:T(1024)(128)(4,1)} %bitcast.388), calls=%async_computation.4 | async-start | bytes 8388608
  287.6 8.5 %slice-start.1 = ((s8[8388608]{0:T(1024)(128)(4,1)}), s8[4194304]{0:T(1024)(128)(4,1)S(1)}, s32[]{:S(2)}) async-start(s8[8388608]{0:T(1024)(128)(4,1)} %bitcast.388), calls=%async_computation.5 | async-start | bytes 8388608
  339.7 3.6 copy-start.1
  366.6 31.3 %copy-start.3 = (bf16[8,64,256]{2,1,0:T(8,128)(2,1)S(1)}, bf16[8,64,256]{2,1,0:T(8,128)(2,1)}, u32[]{:S(2)}) copy-start(bf16[8,64,256]{2,1,0:T(8,128)(2,1)} %param.10) | copy-start | bytes 786436
Sparse Core Ops, SparseCore 0:
  10.0 51.7 all-gather.2
  63.4 200.0 all-gather.4
  366.8 31.1 reduce-scatter.1
where the time goes:
time: 407 us
  waiting for transfers between devices  271 us (67%)
  matrix products  105 us (26%)
  local copies, waits for them, and re-layouts  13.4 us (3%)
  between operations  13.2 us (3%)
    all_gather x1, waiting for transfers between devices, shards(): lax.all_gather(intersections, 'cols', axis=2, tiled=True)  189 us
    dot_general x32, matrix products, shards(): jnp.einsum('pcd,pca->pda', intersections[:, slot_index], projected[:, slo...  64.2 us
    all_gather x1, waiting for transfers between devices, shards(): piece = lax.all_gather(masked, 'pairs', axis=0, tiled=True)  50.1 us
    reduce_scatter x1, waiting for transfers between devices, shards(): lax.psum_scatter(partial_value, 'cols', scatter_dimension=1, tiled=True)  31.3 us
    dot_general x1, matrix products, shards(): jnp.einsum('pab,pbc->pac', fock_cols, masked, preferred_element_type=jnp....  23.3 us
    dot_general x1, matrix products, shards(): jnp.einsum('pqab,pqbc->pqac', partner_blocks, whole_intersections, prefer...  15.6 us
    gather x1, local copies, waits for them, and re-layouts, shards(): picked = piece[jnp.clip(linear, 0, piece.shape[0] - 1)]  12.4 us
  transfers between devices with their start and end apart: 3, of which 3 were waited for; matrix products, arithmetic and copies ran while one was open for 3% of the time, Pallas kernels for 0%

commit v1 on v0

--- a/solution.py
+++ b/solution.py
@@ -17,7 +17,14 @@
     masked = jnp.where(keep, amplitudes, jnp.zeros_like(amplitudes))
     linear = partners.reshape(-1)
     empty = jnp.zeros((local_pairs * CPL, share, width), jnp.bfloat16)
-    piece = lax.all_gather(masked, "pairs", axis=0, tiled=True)
+    ring = [masked]
+    for hop in range(7):
+        ring.append(lax.ppermute(ring[-1], "pairs", [(dev, (dev + 1) % 8) for dev in range(8)]))
+    piece = jnp.roll(
+        jnp.concatenate(ring[::-1], axis=0),
+        (lax.axis_index("pairs") + 1) * ring[0].shape[0],
+        axis=0,
+    )
     present = (linear >= 0) & (linear < piece.shape[0])
     picked = piece[jnp.clip(linear, 0, piece.shape[0] - 1)]
     partner_flat = jnp.where(present[:, None, None], picked, empty)

time: 407 us -> 357 us (0.88)
  waiting for transfers between devices: 271 us -> 222 us
    ppermute x0 -> x7, waiting for transfers between devices: none -> 64.8 us  [shards(): lax.ppermute(ring[-1], 'pairs', [(dev, (dev + 1) % 8) for dev in range(8)])]
    all_gather x1, waiting for transfers between devices: 189 us -> 125 us  [shards(): lax.all_gather(intersections, 'cols', axis=2, tiled=True)]
    all_gather x1 -> x0, waiting for transfers between devices: 50.1 us -> none  [shards(): piece = lax.all_gather(masked, 'pairs', axis=0, tiled=True)]
  transfers between devices with their start and end apart: 3 -> 9, of which waited for: 3 -> 9; matrix products, arithmetic and copies ran while one was open for 3% -> 3% of each run, Pallas kernels for 0% -> 0%
where the time goes in v1:
time: 357 us
  waiting for transfers between devices  222 us (62%)
  matrix products  105 us (29%)
  between operations  13.7 us (4%)
  local copies, waits for them, and re-layouts  12 us (3%)
    all_gather x1, waiting for transfers between devices, shards(): lax.all_gather(intersections, 'cols', axis=2, tiled=True)  125 us
    ppermute x7, waiting for transfers between devices, shards(): lax.ppermute(ring[-1], 'pairs', [(dev, (dev + 1) % 8) for dev in range(8)])  64.8 us
    dot_general x32, matrix products, shards(): jnp.einsum('pcd,pca->pda', intersections[:, slot_index], projected[:, slo...  64.1 us
    reduce_scatter x1, waiting for transfers between devices, shards(): lax.psum_scatter(partial_value, 'cols', scatter_dimension=1, tiled=True)  31.3 us
    dot_general x1, matrix products, shards(): jnp.einsum('pab,pbc->pac', fock_cols, masked, preferred_element_type=jnp....  23.3 us
    dot_general x1, matrix products, shards(): jnp.einsum('pqab,pqbc->pqac', partner_blocks, whole_intersections, prefer...  15.6 us
    gather x1, local copies, waits for them, and re-layouts, shards(): picked = piece[jnp.clip(linear, 0, piece.shape[0] - 1)]  8.59 us
  transfers between devices with their start and end apart: 9, of which 9 were waited for; matrix products, arithmetic and copies ran while one was open for 3% of the time, Pallas kernels for 0%

profile of v1, /device:TPU:0, one launch (start us, length us, event | category | flops | bytes accessed | tf_op | source)
XLA Modules:
  0.0 356.5 jit_solution(10079852008926161571)
XLA Ops:
  6.5 0.0 all-gather.2.cloned.1.call-start
  6.6 0.7 all-gather.2.cloned.1.call-update
  7.3 0.0 reduce-scatter.2.cloned.1.call-start
  7.4 0.1 broadcast_compare_fusion
  7.4 0.1 iota_compare_fusion
  7.5 0.1 copy-done.2
  7.6 0.1 and_select_fusion
  7.7 3.0 collective-permute-start
  10.8 9.3 %collective-permute-done = bf16[8,64,256]{2,1,0:T(8,128)(2,1)S(1)} collective-permute-done((bf16[8,64,256]{2,1,0:T(8,128)(2,1)S(1)}, bf16[8,64,256]{2,1,0:T(8,128)(2,1)S(1)}, u32[]{:S(2)}, u32[]{:S(2)}) %collective-permute-start) | collective-permute-done | bytes 262176 | tf_op jit(solution)/shard_map/ppermute | solution.py:22
  20.1 10.2 %collective-permute-done.1 = bf16[8,64,256]{2,1,0:T(8,128)(2,1)S(1)} collective-permute-done((bf16[8,64,256]{2,1,0:T(8,128)(2,1)S(1)}, bf16[8,64,256]{2,1,0:T(8,128)(2,1)S(1)}, u32[]{:S(2)}, u32[]{:S(2)}) %collective-permute-start.1) | collective-permute-done | bytes 262176 | tf_op jit(solution)/shard_map/ppermute | solution.py:22
  30.3 9.3 %collective-permute-done.2 = bf16[8,64,256]{2,1,0:T(8,128)(2,1)S(1)} collective-permute-done((bf16[8,64,256]{2,1,0:T(8,128)(2,1)S(1)}, bf16[8,64,256]{2,1,0:T(8,128)(2,1)S(1)}, u32[]{:S(2)}, u32[]{:S(2)}) %collective-permute-start.2) | collective-permute-done | bytes 262176 | tf_op jit(solution)/shard_map/ppermute | solution.py:22
  39.6 9.1 %collective-permute-done.3 = bf16[8,64,256]{2,1,0:T(8,128)(2,1)S(1)} collective-permute-done((bf16[8,64,256]{2,1,0:T(8,128)(2,1)S(1)}, bf16[8,64,256]{2,1,0:T(8,128)(2,1)S(1)}, u32[]{:S(2)}, u32[]{:S(2)}) %collective-permute-start.3) | collective-permute-done | bytes 262176 | tf_op jit(solution)/shard_map/ppermute | solution.py:22
  48.7 0.5 slice_reduce_fusion.31
  49.2 8.6 %collective-permute-done.4 = bf16[8,64,256]{2,1,0:T(8,128)(2,1)S(1)} collective-permute-done((bf16[8,64,256]{2,1,0:T(8,128)(2,1)S(1)}, bf16[8,64,256]{2,1,0:T(8,128)(2,1)S(1)}, u32[]{:S(2)}, u32[]{:S(2)}) %collective-permute-start.4) | collective-permute-done | bytes 262176 | tf_op jit(solution)/shard_map/ppermute | solution.py:22
  57.8 0.4 slice_reduce_fusion.30
  58.2 0.1 min.12
  58.2 9.2 %collective-permute-done.5 = bf16[8,64,256]{2,1,0:T(8,128)(2,1)S(1)} collective-permute-done((bf16[8,64,256]{2,1,0:T(8,128)(2,1)S(1)}, bf16[8,64,256]{2,1,0:T(8,128)(2,1)S(1)}, u32[]{:S(2)}, u32[]{:S(2)}) %collective-permute-start.5) | collective-permute-done | bytes 262176 | tf_op jit(solution)/shard_map/ppermute | solution.py:22
  67.5 9.1 %collective-permute-done.6 = bf16[8,64,256]{2,1,0:T(8,128)(2,1)} collective-permute-done((bf16[8,64,256]{2,1,0:T(8,128)(2,1)S(1)}, bf16[8,64,256]{2,1,0:T(8,128)(2,1)}, u32[]{:S(2)}, u32[]{:S(2)}) %collective-permute-start.6) | collective-permute-done | bytes 262176 | tf_op jit(solution)/shard_map/ppermute | solution.py:22
  76.6 1.0 constant_dynamic-update-slice_fusion.15
  77.8 0.1 constant_dynamic-update-slice_fusion.8
  77.9 1.0 constant_dynamic-update-slice_fusion.7
  79.1 0.1 constant_dynamic-update-slice_fusion
  79.2 0.1 constant_dynamic-slice_fusion
  79.4 8.6 %gather_fusion = bf16[256,64,256]{2,1,0:T(8,128)(2,1)} fusion(bf16[64,64,256]{2,1,0:T(8,128)(2,1)S(1)} %constant_dynamic-slice_fusion, s32[1024]{0:T(1024)S(1)} %pad_clamp_fusion), kind=kCustom, calls=%fused_computation | custom fusion | bytes 16778240 | tf_op jit(solution)/shard_map/gather | solution.py:29
  88.0 125.2 %all-gather.2.cloned.1.call-done = bf16[8,32,256,256]{3,2,1,0:T(8,128)(2,1)} async-done(((bf16[8,32,64,256]{3,2,1,0:T(8,128)(2,1)}), bf16[8,32,256,256]{3,2,1,0:T(8,128)(2,1)}) %all-gather.2.cloned.1.call-update) | async-done | bytes 33554448 | tf_op jit(solution)/shard_map/all_gather | solution.py:36
  213.2 15.6 %fusion.3 = bf16[8,32,64,256]{3,2,1,0:T(8,128)(2,1)S(1)} fusion(bf16[8,32,256,256]{3,2,1,0:T(8,128)(2,1)} %all-gather.2.cloned.1.call-done, bf16[8,32,64,256]{3,2,1,0:T(8,128)(2,1)} %bitcast.390, pred[8,32]{1,0:T(8,128)(4,1)S(1)} %compare_and_fusion), kind=kOutput, calls=%fused_computation.4 | convolution fusion | flops 2155872256 | bytes 50331904 | tf_op jit(solution)/shard_map/pqab,pqbc->pqac/dot_general | solution.py:37
  228.8 0.0 slice-start
  228.8 2.9 fusion.11
  231.7 2.8 fusion.12
  234.5 2.7 fusion.13
  237.2 2.9 fusion.14
  240.2 2.8 fusion.15
  242.9 2.8 fusion.16
  245.8 1.8 fusion.17
  247.6 1.8 fusion.18
  249.4 1.8 fusion.19
  251.2 1.8 fusion.20
  253.1 1.8 fusion.21
  254.8 1.8 fusion.22
  256.7 1.8 fusion.23
  258.5 1.9 fusion.24
  260.4 1.8 fusion.25
  262.1 1.8 fusion.26
  264.0 1.8 fusion.27
  265.8 1.8 fusion.28
  267.6 1.9 fusion.29
  269.4 1.8 fusion.30
  271.2 1.8 fusion.31
  273.0 1.8 fusion.32
  274.8 1.8 fusion.33
  276.6 1.8 fusion.34
  278.5 1.8 fusion.35
  280.3 1.8 fusion.36
  282.1 1.9 fusion.37
  283.9 1.8 fusion.38
  285.7 1.8 fusion.39
  287.5 1.8 fusion.40
  289.3 1.8 fusion.41
  291.1 1.8 fusion.42
  293.0 23.3 %bitcast_add_fusion = f32[8,256,256]{2,1,0:T(8,128)} fusion(f32[8,256,256]{1,2,0:T(8,128)} %fusion.11, f32[8,256,256]{1,2,0:T(8,128)} %fusion.12, f32[8,256,256]{1,2,0:T(8,128)} %fusion.13, f32[8,256,256]{1,2,0:T(8,128)} %fusion.14, f32[8,256,256]{1,2,0:T(8,128)} %fusion.15, f32[8,256,256]{1,2,0:T(8,128)} %fusion.16, f32[8,256,256]{1,2,0:T(8,128)} %fusion.17, ...), kind=kOutput, calls=%fused_computation.6 | convolution fusion | flops 100663296 | bytes 70008832 | tf_op jit(solution)/shard_map/pab,pbc->pac/dot_general | solution.py:33
  316.2 0.0 copy-start.3
  316.2 0.0 reduce-scatter.2.cloned.1.call-update
  316.3 31.3 %reduce-scatter.2.cloned.1.call-done = f32[8,64,256]{2,1,0:T(8,128)} async-done(((f32[8,256,256]{2,1,0:T(8,128)}), f32[8,64,256]{2,1,0:T(8,128)}) %reduce-scatter.2.cloned.1.call-update) | async-done | bytes 524304 | tf_op jit(solution)/shard_map/reduce_scatter | solution.py:48
  347.6 2.1 fusion.9
  (37 shorter events, 0.3 us)
Async XLA Ops:
  6.5 286.4 %copy-start = (bf16[8,256,256]{2,1,0:T(8,128)(2,1)S(1)}, bf16[8,256,256]{2,1,0:T(8,128)(2,1)}, u32[]{:S(2)}) copy-start(bf16[8,256,256]{2,1,0:T(8,128)(2,1)} %param.9) | copy-start | bytes 3145732
  6.5 0.8 copy-start.5
  6.5 1.1 copy-start.2
  6.5 42.1 %copy-start.1 = (f32[8,32]{1,0:T(8,128)S(1)}, f32[8,32]{1,0:T(8,128)}, u32[]{:S(2)}) copy-start(f32[8,32]{1,0:T(8,128)} %param.13) | copy-start | bytes 3076
  6.5 42.6 %copy-start.4 = (s32[8,32]{1,0:T(8,128)S(1)}, s32[8,32]{1,0:T(8,128)}, u32[]{:S(2)}) copy-start(s32[8,32]{1,0:T(8,128)} %param.12) | copy-start | bytes 3076
  6.5 206.6 %all-gather.2.cloned.1.call-start = ((), (), s32[]{:S(2)}) async-start(), calls=%async_computation.1 | async-start | bytes 41943040 | tf_op jit(solution)/shard_map/all_gather | solution.py:36
  7.3 340.3 %reduce-scatter.2.cloned.1.call-start = ((), (), s32[]{:S(2)}) async-start(), calls=%async_computation.2 | async-start | bytes 2621440 | tf_op jit(solution)/shard_map/reduce_scatter | solution.py:48
  7.7 12.4 %collective-permute-start = (bf16[8,64,256]{2,1,0:T(8,128)(2,1)S(1)}, bf16[8,64,256]{2,1,0:T(8,128)(2,1)S(1)}, u32[]{:S(2)}, u32[]{:S(2)}) collective-permute-start(bf16[8,64,256]{2,1,0:T(8,128)(2,1)S(1)} %and_select_fusion), channel_id=1, source_target_pairs={{0,4},{4,8},{8,12},{12,16},{16,20},{20,24},{24,28},{28,0},{1,5},{5... | collective-permute-start | bytes 786440 | tf_op jit(solution)/shard_map/ppermute | solution.py:22
  20.1 10.2 %collective-permute-start.1 = (bf16[8,64,256]{2,1,0:T(8,128)(2,1)S(1)}, bf16[8,64,256]{2,1,0:T(8,128)(2,1)S(1)}, u32[]{:S(2)}, u32[]{:S(2)}) collective-permute-start(bf16[8,64,256]{2,1,0:T(8,128)(2,1)S(1)} %collective-permute-done), channel_id=1, source_target_pairs={{0,4},{4,8},{8,12},{12,16},{16,20},{20,24},{24,28},{28,0},{1,5},{5... | collective-permute-start | bytes 786440 | tf_op jit(solution)/shard_map/ppermute | solution.py:22
  30.3 9.3 %collective-permute-start.2 = (bf16[8,64,256]{2,1,0:T(8,128)(2,1)S(1)}, bf16[8,64,256]{2,1,0:T(8,128)(2,1)S(1)}, u32[]{:S(2)}, u32[]{:S(2)}) collective-permute-start(bf16[8,64,256]{2,1,0:T(8,128)(2,1)S(1)} %collective-permute-done.1), channel_id=1, source_target_pairs={{0,4},{4,8},{8,12},{12,16},{16,20},{20,24},{24,28},{28,0},{1,5},{5... | collective-permute-start | bytes 786440 | tf_op jit(solution)/shard_map/ppermute | solution.py:22
  39.6 9.1 %collective-permute-start.3 = (bf16[8,64,256]{2,1,0:T(8,128)(2,1)S(1)}, bf16[8,64,256]{2,1,0:T(8,128)(2,1)S(1)}, u32[]{:S(2)}, u32[]{:S(2)}) collective-permute-start(bf16[8,64,256]{2,1,0:T(8,128)(2,1)S(1)} %collective-permute-done.2), channel_id=1, source_target_pairs={{0,4},{4,8},{8,12},{12,16},{16,20},{20,24},{24,28},{28,0},{1,5},{5... | collective-permute-start | bytes 786440 | tf_op jit(solution)/shard_map/ppermute | solution.py:22
  48.7 9.1 %collective-permute-start.4 = (bf16[8,64,256]{2,1,0:T(8,128)(2,1)S(1)}, bf16[8,64,256]{2,1,0:T(8,128)(2,1)S(1)}, u32[]{:S(2)}, u32[]{:S(2)}) collective-permute-start(bf16[8,64,256]{2,1,0:T(8,128)(2,1)S(1)} %collective-permute-done.3), channel_id=1, source_target_pairs={{0,4},{4,8},{8,12},{12,16},{16,20},{20,24},{24,28},{28,0},{1,5},{5... | collective-permute-start | bytes 786440 | tf_op jit(solution)/shard_map/ppermute | solution.py:22
  57.8 9.7 %collective-permute-start.5 = (bf16[8,64,256]{2,1,0:T(8,128)(2,1)S(1)}, bf16[8,64,256]{2,1,0:T(8,128)(2,1)S(1)}, u32[]{:S(2)}, u32[]{:S(2)}) collective-permute-start(bf16[8,64,256]{2,1,0:T(8,128)(2,1)S(1)} %collective-permute-done.4), channel_id=1, source_target_pairs={{0,4},{4,8},{8,12},{12,16},{16,20},{20,24},{24,28},{28,0},{1,5},{5... | collective-permute-start | bytes 786440 | tf_op jit(solution)/shard_map/ppermute | solution.py:22
  67.4 9.2 %collective-permute-start.6 = (bf16[8,64,256]{2,1,0:T(8,128)(2,1)S(1)}, bf16[8,64,256]{2,1,0:T(8,128)(2,1)}, u32[]{:S(2)}, u32[]{:S(2)}) collective-permute-start(bf16[8,64,256]{2,1,0:T(8,128)(2,1)S(1)} %collective-permute-done.5), channel_id=1, source_target_pairs={{0,4},{4,8},{8,12},{12,16},{16,20},{20,24},{24,28},{28,0},{1,5},{5... | collective-permute-start | bytes 786440 | tf_op jit(solution)/shard_map/ppermute | solution.py:22
  228.8 17.0 %slice-start = ((s8[8388608]{0:T(1024)(128)(4,1)}), s8[4194304]{0:T(1024)(128)(4,1)S(1)}, s32[]{:S(2)}) async-start(s8[8388608]{0:T(1024)(128)(4,1)} %bitcast.388), calls=%async_computation.3 | async-start | bytes 8388608
  237.2 8.6 %slice-start.1 = ((s8[8388608]{0:T(1024)(128)(4,1)}), s8[4194304]{0:T(1024)(128)(4,1)S(1)}, s32[]{:S(2)}) async-start(s8[8388608]{0:T(1024)(128)(4,1)} %bitcast.388), calls=%async_computation.4 | async-start | bytes 8388608
  316.2 31.4 %copy-start.3 = (bf16[8,64,256]{2,1,0:T(8,128)(2,1)S(1)}, bf16[8,64,256]{2,1,0:T(8,128)(2,1)}, u32[]{:S(2)}) copy-start(bf16[8,64,256]{2,1,0:T(8,128)(2,1)} %param.10) | copy-start | bytes 786436
Sparse Core Ops, SparseCore 0:
  8.9 204.2 all-gather.1
  316.4 31.1 reduce-scatter.1
